TPU v7x, 32 devices: a whole 2x2x4 slice. The times are simulated.
32 devices in a mesh: ctx: 4 (over x, core), exp: 8 (over z, y).
Axes of the slice: x: 2, y: 2, z: 4, core: 2. Of those that a mesh axis runs over, the one named last changes fastest.
Arguments:
- q_nope: bfloat16 [128, 128, 512], P('ctx', 'exp'), may hold values from -72 to 72
- q_rope: bfloat16 [128, 8192], P('ctx', 'exp'), may hold values from -6 to 6
- cache_keys: bfloat16 [576, 512], P(None, 'ctx'), may hold values from -6 to 6
- fresh_keys: bfloat16 [576, 128], P(None, 'ctx'), may hold values from -6 to 6
- block_order: int32 [8], replicated, may hold values from 0 to 7, each once
- w_uv: bfloat16 [128, 512, 128], P('exp'), may hold values from -0.25 to 0.25
- w_out: bfloat16 [16384, 7168], P('exp', 'ctx'), may hold values from -0.046875 to 0.046875
- residual: bfloat16 [128, 7168], P(('ctx', 'exp')), may hold values from -6 to 6
- norm_gain: float32 [7168], replicated, may hold values from 0.5 to 1.5
- router_weight: bfloat16 [7168, 16], replicated, may hold values from -0.0625 to 0.0625
- expert_ids: int32 [128, 8], P(('ctx', 'exp')), may hold values from 0 to 15, all different within a row; in each aligned block of 4 rows (0 to 3, 4 to 7, ...) at most 3 rows name the same one
- w_gate: bfloat16 [16, 7168, 2048], P('exp', None, 'ctx'), may hold values from -0.0625 to 0.0625
- w_up: bfloat16 [16, 7168, 2048], P('exp', None, 'ctx'), may hold values from -0.0625 to 0.0625
- w_down: bfloat16 [16, 2048, 7168], P('exp', 'ctx'), may hold values from -0.125 to 0.125
Outputs:
- layer_out: bfloat16 [128, 7168], P(('ctx', 'exp'))
Inputs may be any that keep to these rules, and one draw needn't show every extreme that they name: A permutation: block j of the new tokens (16 rows) sits at positions 512 + block_order[j] * 16 onward. `expert_ids`: each row names 8 different experts; the 4 rows of one device name no expert more than 3 times, and in some aligned block one expert exactly 3 times.
All inputs are finite; a program needn't handle non-finite values.
Results may differ from a plain program's by a relative error of at most 0.012.
Values may be sent and summed in bfloat16 or wider, within the bound.
A program may use at most 128 MiB of HBM per device.

v0:
```python
import math
import jax
import jax.numpy as jnp
from jax import lax
from jax.sharding import PartitionSpec as P

QKD = 192
CAP = 3
ROUTE_SCALE = 2.5
NORM_EPS = 1e-06


def block_position(row_index, block_order, block_rows):
    blocks = row_index // block_rows
    lookup = blocks[:, None] == jnp.arange(block_order.shape[0], dtype=jnp.int32)[None, :]
    leading = jnp.sum(jnp.where(lookup, block_order[None, :], 0), axis=1)
    return leading * block_rows + row_index % block_rows


def attend(query_lat, query_pe, keys, visible):
    row_count, head_count, latent_width = query_lat.shape
    key_count = keys.shape[1]
    pe_width = query_pe.shape[1] // head_count
    first_dot = jnp.dot(
        query_lat.reshape(row_count * head_count, latent_width),
        keys[:latent_width],
        preferred_element_type=jnp.float32,
    )
    second_dot = jnp.dot(
        query_pe.reshape(row_count * head_count, pe_width),
        keys[latent_width:],
        preferred_element_type=jnp.float32,
    )
    scores = ((first_dot + second_dot) * (1.0 / math.sqrt(QKD))).reshape(
        row_count, head_count, key_count
    )
    scores = jnp.where(visible[:, None, :], scores, -jnp.inf)
    row_max = jnp.max(scores, axis=2)
    exponent = jnp.exp(scores - row_max[:, :, None])
    row_sum = jnp.sum(exponent, axis=2)
    weights = exponent.astype(jnp.bfloat16).reshape(row_count * head_count, key_count)
    latent = lax.dot_general(
        weights, keys[:latent_width], (((1,), (1,)), ((), ())), preferred_element_type=jnp.float32
    )
    return (row_max, row_sum, latent.reshape(row_count, head_count, latent_width))


def merge_partial(earlier, latter):
    highest = latter[0]
    earlier_scale = jnp.exp(earlier[0] - highest)
    latter_scale = jnp.exp(latter[0] - highest)
    row_sum = earlier_scale * earlier[1] + latter_scale * latter[1]
    latent = earlier_scale[:, :, None] * earlier[2] + latter_scale[:, :, None] * latter[2]
    return (highest, row_sum, latent)


def body(
    q_nope,
    q_rope,
    cache_keys,
    fresh_keys,
    block_order,
    w_uv,
    w_out,
    residual,
    norm_gain,
    router_weight,
    expert_ids,
    w_gate,
    w_up,
    w_down,
):
    ctx_count = lax.axis_size("ctx")
    exp_count = lax.axis_size("exp")
    ctx_index = lax.axis_index("ctx")
    rows_here, heads_here, latent_width = q_nope.shape
    value_width = w_uv.shape[2]
    cache_len = cache_keys.shape[1]
    key_cols = cache_len + rows_here
    block_rows = rows_here // 2
    keys_here = jnp.concatenate([cache_keys, fresh_keys], axis=1)
    w_uv_wide = w_uv.astype(jnp.float32)
    own_rows = ctx_index * rows_here + jnp.arange(rows_here, dtype=jnp.int32)
    own_pos = block_position(own_rows, block_order, block_rows)
    start_state = (
        jnp.full((rows_here, heads_here), -jnp.inf, jnp.float32),
        jnp.zeros((rows_here, heads_here), jnp.float32),
        jnp.zeros((rows_here, heads_here, latent_width), jnp.float32),
    )
    portion = lax.all_gather(keys_here, "ctx", axis=1, tiled=True)
    columns = jnp.arange(portion.shape[1], dtype=jnp.int32)
    owner_dev = columns // key_cols
    within = columns % key_cols
    fresh_row = owner_dev * rows_here + within - cache_len
    key_pos = jnp.where(within < cache_len, -1, block_position(fresh_row, block_order, block_rows))
    visible = key_pos[None, :] <= own_pos[:, None]
    row_max, row_sum, latent = merge_partial(start_state, attend(q_nope, q_rope, portion, visible))
    normal_lat = latent / row_sum[:, :, None]
    head_wide = jnp.einsum("rhl,hlv->rhv", normal_lat, w_uv_wide, precision=lax.Precision.HIGHEST)
    head_out = head_wide.astype(jnp.bfloat16).reshape(rows_here, heads_here * value_width)
    tok_here, model_width = residual.shape
    col_part = w_out.shape[1]
    head_partial = jnp.dot(
        lax.all_gather(head_out, "ctx", axis=0, tiled=True),
        w_out,
        preferred_element_type=jnp.float32,
    )
    arranged = head_partial.reshape(ctx_count, exp_count, tok_here, col_part)
    head_total = lax.psum_scatter(
        arranged.astype(jnp.bfloat16), "exp", scatter_dimension=1, tiled=True
    )
    attention = lax.all_to_all(head_total, "ctx", split_axis=0, concat_axis=3, tiled=True).reshape(
        tok_here, model_width
    )
    hidden = residual.astype(jnp.float32) + attention.astype(jnp.float32)
    mean_square = jnp.mean(hidden * hidden, axis=1, keepdims=True)
    normed = (hidden * lax.rsqrt(mean_square + NORM_EPS) * norm_gain).astype(jnp.bfloat16)
    affinity = jax.nn.sigmoid(jnp.dot(normed, router_weight, preferred_element_type=jnp.float32))
    expert_count = router_weight.shape[1]
    onehot = expert_ids[:, :, None] == jnp.arange(expert_count, dtype=jnp.int32)[None, None, :]
    chosen = jnp.sum(jnp.where(onehot, affinity[:, None, :], 0.0), axis=2)
    route = ROUTE_SCALE * chosen / jnp.sum(chosen, axis=1, keepdims=True)
    mixing = jnp.sum(jnp.where(onehot, route[:, :, None], 0.0), axis=1)
    picked = jnp.sum(onehot.astype(jnp.int32), axis=1)
    slot_index = jnp.cumsum(picked, axis=0) - picked
    slot_hot = (slot_index[:, :, None] == jnp.arange(CAP, dtype=jnp.int32)[None, None, :]) & (
        picked[:, :, None] > 0
    )
    dispatch_map = (
        jnp.transpose(slot_hot, (1, 2, 0))
        .reshape(expert_count * CAP, tok_here)
        .astype(jnp.bfloat16)
    )
    send_rows = jnp.dot(dispatch_map, normed, preferred_element_type=jnp.float32).astype(
        jnp.bfloat16
    )
    arrived = lax.all_to_all(
        send_rows.reshape(expert_count, CAP, model_width),
        "exp",
        split_axis=0,
        concat_axis=1,
        tiled=True,
    )
    local_experts = arrived.shape[0]
    portion = lax.all_gather(arrived, "ctx", axis=1, tiled=True)
    gate = jnp.einsum("end,edf->enf", portion, w_gate, preferred_element_type=jnp.float32)
    upward = jnp.einsum("end,edf->enf", portion, w_up, preferred_element_type=jnp.float32)
    activations = (jax.nn.silu(gate) * upward).astype(jnp.bfloat16)
    expert_total = lax.psum_scatter(
        jnp.einsum("enf,efd->ned", activations, w_down, preferred_element_type=jnp.float32).astype(
            jnp.bfloat16
        ),
        "ctx",
        scatter_dimension=0,
        tiled=True,
    )
    going_back = expert_total.reshape(exp_count, CAP, local_experts, model_width)
    returned = lax.all_to_all(going_back, "exp", split_axis=0, concat_axis=2, tiled=True)
    combine_map = jnp.where(slot_hot, mixing[:, :, None], 0.0)
    combine_map = jnp.transpose(combine_map, (0, 2, 1)).reshape(tok_here, CAP * expert_count)
    mixture = jnp.dot(
        combine_map,
        returned.reshape(CAP * expert_count, model_width).astype(jnp.float32),
        precision=lax.Precision.HIGHEST,
    )
    return (hidden + mixture).astype(jnp.bfloat16)


def solution(mesh):
    return jax.shard_map(
        body,
        mesh=mesh,
        in_specs=(
            P("ctx", "exp", None),
            P("ctx", "exp"),
            P(None, "ctx"),
            P(None, "ctx"),
            P(),
            P("exp", None, None),
            P("exp", "ctx"),
            P(("ctx", "exp"), None),
            P(),
            P(),
            P(("ctx", "exp"), None),
            P("exp", None, "ctx"),
            P("exp", None, "ctx"),
            P("exp", "ctx", None),
        ),
        out_specs=P(("ctx", "exp"), None),
        check_vma=False,
    )
```

profile of v0, /device:TPU:0, one launch (start us, length us, event | category | flops | bytes accessed | tf_op | source)
XLA Modules:
  0.0 268.8 jit_solution(8497776579315052715)
XLA Ops:
  6.6 0.9 select_reduce_fusion.4
  7.5 0.7 select_reduce_fusion.2
  8.2 1.0 reshape.299
  9.2 1.1 copy.39
  10.3 0.8 pad_maximum_fusion
  11.1 10.3 %all_gather.9 = bf16[576,640]{0,1:T(8,128)(2,1)S(1)} all-gather(bf16[576,160]{0,1:T(8,128)(2,1)S(1)} %pad_maximum_fusion), channel_id=1, replica_groups=mesh['ctx'=4,'exp'=8] {'ctx'}, dimensions={1}, use_global_device_ids=true | all-gather | bytes 921600 | tf_op jit(solution)/shard_map/all_gather | solution.py:90
  21.4 1.6 fusion.16
  23.1 0.1 broadcast_in_dim.113
  23.2 0.5 fusion.39
  23.7 1.1 fusion.8
  25.3 1.7 fusion.6
  27.0 1.0 fusion.10
  28.1 7.3 %all_gather.10 = bf16[128,2048]{1,0:T(8,128)(2,1)S(1)} all-gather(bf16[32,2048]{1,0:T(8,128)(2,1)S(1)} %bitcast.75), channel_id=1, replica_groups=mesh['ctx'=4,'exp'=8] {'ctx'}, dimensions={0}, use_global_device_ids=true | all-gather | bytes 655360 | tf_op jit(solution)/shard_map/all_gather | solution.py:104
  35.3 4.2 %convolution_convert_fusion.2 = bf16[128,1792]{1,0:T(8,128)(2,1)S(1)} fusion(bf16[128,2048]{1,0:T(8,128)(2,1)S(1)} %all_gather.10, bf16[2048,1792]{1,0:T(8,128)(2,1)} %param.20), kind=kOutput, calls=%fused_computation.5 | convolution fusion | flops 939753472 | bytes 8323072 | tf_op jit(solution)/shard_map/dot_general | solution.py:103
  39.6 0.9 convert_element_type.60
  40.5 0.6 dynamic-slice
  41.1 0.1 convert_reduce_fusion
  41.2 72.6 %all-reduce.3.cloned.1.call-done = bf16[4,8,4,1792]{3,2,1,0:T(4,128)(2,1)} async-done(((bf16[4,8,4,1792]{3,2,1,0:T(4,128)(2,1)}), bf16[4,8,4,1792]{3,2,1,0:T(4,128)(2,1)}) %all-reduce.3.cloned.1.call-update) | async-done | bytes 458768
  113.9 2.1 constant_dynamic-slice_fusion
  115.9 3.3 %all-to-all-start = ((bf16[4,1,4,1792]{3,2,1,0:T(4,128)(2,1)}), bf16[4,1,4,1792]{3,2,1,0:T(4,128)(2,1)S(1)}, u32[]{:S(2)}, u32[]{:S(2)}) async-start(bf16[4,1,4,1792]{3,2,1,0:T(4,128)(2,1)} %constant_dynamic-slice_fusion), calls=%async_computation | async-start | bytes 114688 | tf_op jit(solution)/shard_map/all_to_all | solution.py:112
  119.4 0.1 and.113
  119.5 0.1 eq.95
  119.7 0.1 eq.93
  119.8 3.5 %all-to-all-done = bf16[4,1,4,1792]{3,2,1,0:T(4,128)(2,1)S(1)} async-done(((bf16[4,1,4,1792]{3,2,1,0:T(4,128)(2,1)}), bf16[4,1,4,1792]{3,2,1,0:T(4,128)(2,1)S(1)}, u32[]{:S(2)}, u32[]{:S(2)}) %all-to-all-start) | async-done | bytes 57376 | tf_op jit(solution)/shard_map/all_to_all | solution.py:112
  123.3 0.2 multiply_reduce_fusion
  123.5 0.1 multiply_convert_fusion
  123.6 0.3 copy-done.3
  123.9 0.4 convolution_convert_fusion.1
  124.3 0.4 reshape.301
  124.8 26.9 %all_to_all.42 = bf16[16,3,7168]{2,1,0:T(4,128)(2,1)S(1)} all-to-all(bf16[16,3,7168]{2,1,0:T(4,128)(2,1)S(1)} %reshape.301), channel_id=1, replica_groups=mesh['ctx'=4,'exp'=8] {'exp'}, dimensions={0} | all-to-all | bytes 1376256 | tf_op jit(solution)/shard_map/all_to_all | solution.py:137
  151.6 0.6 copy.46
  152.2 1.0 copy.47
  153.2 0.2 reduce-scatter.5.cloned.1.call-start
  153.5 23.9 %all-gather.2.cloned.1.call-done = bf16[2,96,7168]{2,1,0:T(8,128)(2,1)} async-done(((bf16[2,24,7168]{2,1,0:T(8,128)(2,1)}), bf16[2,96,7168]{2,1,0:T(8,128)(2,1)}) %all-gather.2.cloned.1.call-update) | async-done | bytes 2752528 | tf_op jit(solution)/shard_map/all_gather | solution.py:145
  177.4 8.6 %fusion.40 = f32[2,96,512]{2,1,0:T(8,128)S(1)} fusion(bf16[2,96,7168]{2,1,0:T(8,128)(2,1)} %all-gather.2.cloned.1.call-done, bf16[2,7168,512]{2,1,0:T(8,128)(2,1)} %param.25), kind=kOutput, calls=%fused_computation.91 | convolution fusion | flops 1409286144 | bytes 17825792 | tf_op jit(solution)/shard_map/end,edf->enf/dot_general | solution.py:146
  186.0 7.8 %fusion.7 = bf16[2,96,512]{2,1,0:T(8,128)(2,1)S(1)} fusion(bf16[2,96,7168]{2,1,0:T(8,128)(2,1)S(1)} %copy-done.2, bf16[2,7168,512]{2,1,0:T(8,128)(2,1)} %param.26, f32[2,96,512]{2,1,0:T(8,128)S(1)} %fusion.40), kind=kOutput, calls=%fused_computation.15 | convolution fusion | flops 1409875968 | bytes 18022400 | tf_op jit(solution)/shard_map/end,edf->enf/dot_general | solution.py:147
  193.8 2.6 fusion
  196.4 1.8 copy.56
  198.2 35.5 %reduce-scatter.5.cloned.1.call-done = bf16[24,14336]{1,0:T(8,128)(2,1)} async-done(((bf16[96,14336]{1,0:T(8,128)(2,1)}), bf16[24,14336]{1,0:T(8,128)(2,1)}) %reduce-scatter.5.cloned.1.call-update) | async-done | bytes 688144
  233.7 2.6 reshape.310
  236.3 5.5 %all-to-all-start.2 = ((bf16[8,3,2,7168]{3,2,1,0:T(2,128)(2,1)}), bf16[8,3,2,7168]{3,2,1,0:T(2,128)(2,1)S(1)}, u32[]{:S(2)}, u32[]{:S(2)}) async-start(bf16[8,3,2,7168]{3,2,1,0:T(2,128)(2,1)} %bitcast.15), calls=%async_computation.2 | async-start | bytes 1376256 | tf_op jit(solution)/shard_map/all_to_all | solution.py:158
  241.8 0.2 fusion.13
  242.0 0.2 select_reduce_fusion
  242.3 0.1 select_reduce_fusion.3
  242.5 17.2 %all-to-all-done.2 = bf16[8,3,2,7168]{3,2,1,0:T(2,128)(2,1)S(1)} async-done(((bf16[8,3,2,7168]{3,2,1,0:T(2,128)(2,1)}), bf16[8,3,2,7168]{3,2,1,0:T(2,128)(2,1)S(1)}, u32[]{:S(2)}, u32[]{:S(2)}) %all-to-all-start.2) | async-done | bytes 688160 | tf_op jit(solution)/shard_map/all_to_all | solution.py:158
  259.7 0.5 copy.49
  260.1 0.3 reshape.303
  260.4 1.9 fusion.1
  (57 shorter events, 1.2 us)
Async XLA Ops:
  6.5 20.5 %copy-start = (bf16[16,512,128]{2,1,0:T(8,128)(2,1)S(1)}, bf16[16,512,128]{2,1,0:T(8,128)(2,1)}, u32[]{:S(2)}) copy-start(bf16[16,512,128]{2,1,0:T(8,128)(2,1)} %param.19) | copy-start | bytes 6291460
  6.5 107.3 %all-reduce.3.cloned.1.call-start = ((), (), s32[]{:S(2)}) async-start(), calls=%async_computation.6 | async-start | bytes 917504
  35.3 5.2 %copy-start.8 = (u32[32]{0:T(128)S(1)}, u32[32]{0:T(128)}, u32[]{:S(2)}) copy-start(u32[32]{0:T(128)} %constant.104) | copy-start | bytes 388
  35.3 5.8 %copy-start.6 = (s32[4,8]{1,0:T(4,128)S(1)}, s32[4,8]{1,0:T(4,128)}, u32[]{:S(2)}) copy-start(s32[4,8]{1,0:T(4,128)} %param.24) | copy-start | bytes 388
  35.3 87.9 %copy-start.4 = (bf16[4,7168]{1,0:T(4,128)(2,1)S(1)}, bf16[4,7168]{1,0:T(4,128)(2,1)}, u32[]{:S(2)}) copy-start(bf16[4,7168]{1,0:T(4,128)(2,1)} %param.21) | copy-start | bytes 172036
  35.3 88.1 %copy-start.5 = (f32[7168]{0:T(1024)S(1)}, f32[7168]{0:T(1024)}, u32[]{:S(2)}) copy-start(f32[7168]{0:T(1024)} %param.22) | copy-start | bytes 86020
  115.9 7.3 %all-to-all-start = ((bf16[4,1,4,1792]{3,2,1,0:T(4,128)(2,1)}), bf16[4,1,4,1792]{3,2,1,0:T(4,128)(2,1)S(1)}, u32[]{:S(2)}, u32[]{:S(2)}) async-start(bf16[4,1,4,1792]{3,2,1,0:T(4,128)(2,1)} %constant_dynamic-slice_fusion), calls=%async_computation | async-start | bytes 114688 | tf_op jit(solution)/shard_map/all_to_all | solution.py:112
  119.2 58.2 %all-gather.2.cloned.1.call-start = ((), (), s32[]{:S(2)}) async-start(), calls=%async_computation.4 | async-start | bytes 3440640 | tf_op jit(solution)/shard_map/all_gather | solution.py:145
  123.3 0.7 copy-start.3
  153.2 80.5 %reduce-scatter.5.cloned.1.call-start = ((), (), s32[]{:S(2)}) async-start(), calls=%async_computation.5 | async-start | bytes 3440640
  177.4 8.6 %copy-start.2 = (bf16[2,96,7168]{2,1,0:T(8,128)(2,1)S(1)}, bf16[2,96,7168]{2,1,0:T(8,128)(2,1)}, u32[]{:S(2)}) copy-start(bf16[2,96,7168]{2,1,0:T(8,128)(2,1)} %all-gather.2.cloned.1.call-done) | copy-start | bytes 8257540
  177.4 16.4 %slice-start = ((s8[14680064]{0:T(1024)(128)(4,1)}), s8[4194304]{0:T(1024)(128)(4,1)S(1)}, s32[]{:S(2)}) async-start(s8[14680064]{0:T(1024)(128)(4,1)} %bitcast.63), calls=%async_computation.7 | async-start | bytes 8388608
  177.4 16.4 %slice-start.1 = ((s8[14680064]{0:T(1024)(128)(4,1)}), s8[4194304]{0:T(1024)(128)(4,1)S(1)}, s32[]{:S(2)}) async-start(s8[14680064]{0:T(1024)(128)(4,1)} %bitcast.63), calls=%async_computation.8 | async-start | bytes 8388608
  186.0 7.8 %slice-start.2 = ((s8[14680064]{0:T(1024)(128)(4,1)}), s8[4194304]{0:T(1024)(128)(4,1)S(1)}, s32[]{:S(2)}) async-start(s8[14680064]{0:T(1024)(128)(4,1)} %bitcast.63), calls=%async_computation.9 | async-start | bytes 8388608
  186.0 7.8 %slice-start.3 = ((s8[14680064]{0:T(1024)(128)(4,1)}), s8[2097152]{0:T(1024)(128)(4,1)S(1)}, s32[]{:S(2)}) async-start(s8[14680064]{0:T(1024)(128)(4,1)} %bitcast.63), calls=%async_computation.10 | async-start | bytes 4194304
  198.2 43.6 %copy-start.7 = (bf16[7168,16]{0,1:T(8,128)(2,1)S(1)}, bf16[7168,16]{0,1:T(8,128)(2,1)}, u32[]{:S(2)}) copy-start(bf16[7168,16]{0,1:T(8,128)(2,1)} %param.23) | copy-start | bytes 688132
  233.7 28.6 %copy-start.1 = (bf16[16,512,128]{2,1,0:T(8,128)(2,1)S(1)}, bf16[16,512,128]{2,1,0:T(8,128)(2,1)}, u32[]{:S(2)}) copy-start(bf16[16,512,128]{2,1,0:T(8,128)(2,1)} %param.19) | copy-start | bytes 6291460
  236.3 23.4 %all-to-all-start.2 = ((bf16[8,3,2,7168]{3,2,1,0:T(2,128)(2,1)}), bf16[8,3,2,7168]{3,2,1,0:T(2,128)(2,1)S(1)}, u32[]{:S(2)}, u32[]{:S(2)}) async-start(bf16[8,3,2,7168]{3,2,1,0:T(2,128)(2,1)} %bitcast.15), calls=%async_computation.2 | async-start | bytes 1376256 | tf_op jit(solution)/shard_map/all_to_all | solution.py:158
Sparse Core Ops, SparseCore 0:
  40.6 73.1 all-reduce.2
  153.3 23.9 all-gather.1
  198.3 35.3 reduce-scatter.4
where the time goes:
time: 270 us; the launch traced here: 269 us
  waiting for transfers between devices  153 us (57%)
  blocking collectives  44.4 us (16%)
  matrix products  30.6 us (11%)
  local copies, waits for them, and re-layouts  14.2 us (5%)
  between operations  13.4 us (5%)
  starting transfers between devices  9.06 us (3%)
  other arithmetic  4.49 us (2%)
    unnamed x5, waiting for transfers between devices  108 us
    all_to_all x1, blocking collectives, body(): lax.all_to_all(send_rows.reshape(expert_count, CAP, model_width), 'exp',...  26.9 us
    all_gather x1, waiting for transfers between devices, body(): portion = lax.all_gather(arrived, 'ctx', axis=1, tiled=True)  23.9 us
    all_to_all x1, waiting for transfers between devices, body(): lax.all_to_all(going_back, 'exp', split_axis=0, concat_axis=2, tiled=True)  17.2 us
    all_gather x1, blocking collectives, body(): portion = lax.all_gather(keys_here, 'ctx', axis=1, tiled=True)  10.3 us
    dot_general x1, matrix products, body(): jnp.einsum('end,edf->enf', portion, w_gate, preferred_element_type=jnp.fl...  8.57 us
    dot_general x1, matrix products, body(): jnp.einsum('end,edf->enf', portion, w_up, preferred_element_type=jnp.floa...  7.8 us
    all_gather x1, blocking collectives, body(): lax.all_gather(head_out, 'ctx', axis=0, tiled=True)  7.27 us
  transfers between devices with their start and end apart: 5, of which 5 were waited for; matrix products, arithmetic and copies ran while one was open for 1% of the time, Pallas kernels for 0%

commit v1 on v0

--- a/solution.py
+++ b/solution.py
@@ -134,13 +134,10 @@
     send_rows = jnp.dot(dispatch_map, normed, preferred_element_type=jnp.float32).astype(
         jnp.bfloat16
     )
-    arrived = lax.all_to_all(
-        send_rows.reshape(expert_count, CAP, model_width),
-        "exp",
-        split_axis=0,
-        concat_axis=1,
-        tiled=True,
-    )
+    part = send_rows.reshape(expert_count, CAP, model_width)
+    pieces = jnp.split(part, lax.axis_size("exp"), axis=0)
+    arrived_2 = lax.all_to_all(jnp.stack(pieces), "exp", 0, 0)
+    arrived = jnp.concatenate(arrived_2, axis=1)
     local_experts = arrived.shape[0]
     portion = lax.all_gather(arrived, "ctx", axis=1, tiled=True)
     gate = jnp.einsum("end,edf->enf", portion, w_gate, preferred_element_type=jnp.float32)

time: 270 us -> 265 us (0.981)
  blocking collectives: 44.4 us -> 39.3 us
    all_to_all x1, blocking collectives: 26.9 us -> 21.8 us  [body(): arrived_2 = lax.all_to_all(jnp.stack(pieces), 'exp', 0, 0)]
    unnamed x30 -> x37, local copies, waits for them, and re-layouts: 5.92 us -> 6.41 us
where the time goes in v1:
time: 265 us
  waiting for transfers between devices  153 us (58%)
  blocking collectives  39.3 us (15%)
  matrix products  30.5 us (12%)
  local copies, waits for them, and re-layouts  15.1 us (6%)
  between operations  13.5 us (5%)
  starting transfers between devices  9.06 us (3%)
  other arithmetic  4.49 us (2%)
    unnamed x5, waiting for transfers between devices  108 us
    all_gather x1, waiting for transfers between devices, body(): portion = lax.all_gather(arrived, 'ctx', axis=1, tiled=True)  24 us
    all_to_all x1, blocking collectives, body(): arrived_2 = lax.all_to_all(jnp.stack(pieces), 'exp', 0, 0)  21.8 us
    all_to_all x1, waiting for transfers between devices, body(): lax.all_to_all(going_back, 'exp', split_axis=0, concat_axis=2, tiled=True)  17.2 us
    all_gather x1, blocking collectives, body(): portion = lax.all_gather(keys_here, 'ctx', axis=1, tiled=True)  10.3 us
    dot_general x1, matrix products, body(): jnp.einsum('end,edf->enf', portion, w_gate, preferred_element_type=jnp.fl...  8.57 us
    dot_general x1, matrix products, body(): jnp.einsum('end,edf->enf', portion, w_up, preferred_element_type=jnp.floa...  7.8 us
    all_gather x1, blocking collectives, body(): lax.all_gather(head_out, 'ctx', axis=0, tiled=True)  7.27 us
  transfers between devices with their start and end apart: 5, of which 5 were waited for; matrix products, arithmetic and copies ran while one was open for 1% of the time, Pallas kernels for 0%

profile of v1, /device:TPU:0, one launch (start us, length us, event | category | flops | bytes accessed | tf_op | source)
XLA Modules:
  0.0 264.8 jit_solution(3717937364256054724)
XLA Ops:
  6.6 0.9 select_reduce_fusion.4
  7.5 0.7 select_reduce_fusion.2
  8.2 1.0 reshape.319
  9.2 1.1 copy.39
  10.3 0.8 pad_maximum_fusion
  11.1 10.3 %all_gather.9 = bf16[576,640]{0,1:T(8,128)(2,1)S(1)} all-gather(bf16[576,160]{0,1:T(8,128)(2,1)S(1)} %pad_maximum_fusion), channel_id=1, replica_groups=mesh['ctx'=4,'exp'=8] {'ctx'}, dimensions={1}, use_global_device_ids=true | all-gather | bytes 921600 | tf_op jit(solution)/shard_map/all_gather | solution.py:90
  21.4 1.6 fusion.16
  23.1 0.1 broadcast_in_dim.113
  23.2 0.5 fusion.40
  23.7 1.1 fusion.8
  25.3 1.7 fusion.6
  27.0 1.0 fusion.10
  28.1 7.3 %all_gather.10 = bf16[128,2048]{1,0:T(8,128)(2,1)S(1)} all-gather(bf16[32,2048]{1,0:T(8,128)(2,1)S(1)} %bitcast.73), channel_id=1, replica_groups=mesh['ctx'=4,'exp'=8] {'ctx'}, dimensions={0}, use_global_device_ids=true | all-gather | bytes 655360 | tf_op jit(solution)/shard_map/all_gather | solution.py:104
  35.3 4.2 %convolution_convert_fusion.2 = bf16[128,1792]{1,0:T(8,128)(2,1)S(1)} fusion(bf16[128,2048]{1,0:T(8,128)(2,1)S(1)} %all_gather.10, bf16[2048,1792]{1,0:T(8,128)(2,1)} %param.20), kind=kOutput, calls=%fused_computation.5 | convolution fusion | flops 939753472 | bytes 8323072 | tf_op jit(solution)/shard_map/dot_general | solution.py:103
  39.6 0.9 convert_element_type.60
  40.5 0.6 dynamic-slice
  41.1 0.1 convert_reduce_fusion
  41.2 72.6 %all-reduce.3.cloned.1.call-done = bf16[4,8,4,1792]{3,2,1,0:T(4,128)(2,1)} async-done(((bf16[4,8,4,1792]{3,2,1,0:T(4,128)(2,1)}), bf16[4,8,4,1792]{3,2,1,0:T(4,128)(2,1)}) %all-reduce.3.cloned.1.call-update) | async-done | bytes 458768
  113.9 2.1 constant_dynamic-slice_fusion
  115.9 3.3 %all-to-all-start = ((bf16[4,1,4,1792]{3,2,1,0:T(4,128)(2,1)}), bf16[4,1,4,1792]{3,2,1,0:T(4,128)(2,1)S(1)}, u32[]{:S(2)}, u32[]{:S(2)}) async-start(bf16[4,1,4,1792]{3,2,1,0:T(4,128)(2,1)} %constant_dynamic-slice_fusion), calls=%async_computation | async-start | bytes 114688 | tf_op jit(solution)/shard_map/all_to_all | solution.py:112
  119.4 0.1 and.113
  119.5 0.1 eq.95
  119.7 0.1 eq.93
  119.8 3.5 %all-to-all-done = bf16[4,1,4,1792]{3,2,1,0:T(4,128)(2,1)S(1)} async-done(((bf16[4,1,4,1792]{3,2,1,0:T(4,128)(2,1)}), bf16[4,1,4,1792]{3,2,1,0:T(4,128)(2,1)S(1)}, u32[]{:S(2)}, u32[]{:S(2)}) %all-to-all-start) | async-done | bytes 57376 | tf_op jit(solution)/shard_map/all_to_all | solution.py:112
  123.3 0.2 multiply_reduce_fusion
  123.5 0.5 copy-done.3
  123.9 0.1 multiply_convert_fusion
  124.0 0.4 convolution_convert_fusion.1
  124.4 0.2 fusion.39
  125.6 0.6 copy.46
  126.2 21.8 %all_to_all.29 = bf16[8,2,3,7168]{3,1,2,0:T(2,128)(2,1)S(1)} all-to-all(bf16[8,2,3,7168]{3,1,2,0:T(2,128)(2,1)S(1)} %copy.46), channel_id=1, replica_groups=mesh['ctx'=4,'exp'=8] {'exp'}, dimensions={0} | all-to-all | bytes 1376256 | tf_op jit(solution)/shard_map/all_to_all | solution.py:139
  148.1 1.0 copy.47
  149.1 0.2 reduce-scatter.5.cloned.1.call-start
  149.3 24.0 %all-gather.2.cloned.1.call-done = bf16[2,96,7168]{2,1,0:T(8,128)(2,1)} async-done(((bf16[2,24,7168]{2,1,0:T(8,128)(2,1)}), bf16[2,96,7168]{2,1,0:T(8,128)(2,1)}) %all-gather.2.cloned.1.call-update) | async-done | bytes 2752528 | tf_op jit(solution)/shard_map/all_gather | solution.py:142
  173.3 8.6 %fusion.41 = f32[2,96,512]{2,1,0:T(8,128)S(1)} fusion(bf16[2,96,7168]{2,1,0:T(8,128)(2,1)} %all-gather.2.cloned.1.call-done, bf16[2,7168,512]{2,1,0:T(8,128)(2,1)} %param.25), kind=kOutput, calls=%fused_computation.100 | convolution fusion | flops 1409286144 | bytes 17825792 | tf_op jit(solution)/shard_map/end,edf->enf/dot_general | solution.py:143
  181.9 7.8 %fusion.7 = bf16[2,96,512]{2,1,0:T(8,128)(2,1)S(1)} fusion(bf16[2,96,7168]{2,1,0:T(8,128)(2,1)S(1)} %copy-done.2, bf16[2,7168,512]{2,1,0:T(8,128)(2,1)} %param.26, f32[2,96,512]{2,1,0:T(8,128)S(1)} %fusion.41), kind=kOutput, calls=%fused_computation.15 | convolution fusion | flops 1409875968 | bytes 18022400 | tf_op jit(solution)/shard_map/end,edf->enf/dot_general | solution.py:144
  189.8 2.6 fusion
  192.4 1.8 copy.56
  194.2 35.5 %reduce-scatter.5.cloned.1.call-done = bf16[24,14336]{1,0:T(8,128)(2,1)} async-done(((bf16[96,14336]{1,0:T(8,128)(2,1)}), bf16[24,14336]{1,0:T(8,128)(2,1)}) %reduce-scatter.5.cloned.1.call-update) | async-done | bytes 688144
  229.7 2.6 reshape.331
  232.3 5.5 %all-to-all-start.2 = ((bf16[8,3,2,7168]{3,2,1,0:T(2,128)(2,1)}), bf16[8,3,2,7168]{3,2,1,0:T(2,128)(2,1)S(1)}, u32[]{:S(2)}, u32[]{:S(2)}) async-start(bf16[8,3,2,7168]{3,2,1,0:T(2,128)(2,1)} %bitcast.14), calls=%async_computation.2 | async-start | bytes 1376256 | tf_op jit(solution)/shard_map/all_to_all | solution.py:155
  237.8 0.2 fusion.13
  238.0 0.2 select_reduce_fusion
  238.3 0.1 select_reduce_fusion.3
  238.5 17.2 %all-to-all-done.2 = bf16[8,3,2,7168]{3,2,1,0:T(2,128)(2,1)S(1)} async-done(((bf16[8,3,2,7168]{3,2,1,0:T(2,128)(2,1)}), bf16[8,3,2,7168]{3,2,1,0:T(2,128)(2,1)S(1)}, u32[]{:S(2)}, u32[]{:S(2)}) %all-to-all-start.2) | async-done | bytes 688160 | tf_op jit(solution)/shard_map/all_to_all | solution.py:155
  255.6 0.5 copy.49
  256.1 0.3 reshape.324
  256.4 1.9 fusion.1
  (73 shorter events, 2.2 us)
Async XLA Ops:
  6.5 20.5 %copy-start = (bf16[16,512,128]{2,1,0:T(8,128)(2,1)S(1)}, bf16[16,512,128]{2,1,0:T(8,128)(2,1)}, u32[]{:S(2)}) copy-start(bf16[16,512,128]{2,1,0:T(8,128)(2,1)} %param.19) | copy-start | bytes 6291460
  6.5 107.3 %all-reduce.3.cloned.1.call-start = ((), (), s32[]{:S(2)}) async-start(), calls=%async_computation.6 | async-start | bytes 917504
  35.3 5.2 %copy-start.8 = (u32[32]{0:T(128)S(1)}, u32[32]{0:T(128)}, u32[]{:S(2)}) copy-start(u32[32]{0:T(128)} %constant.104) | copy-start | bytes 388
  35.3 5.8 %copy-start.6 = (s32[4,8]{1,0:T(4,128)S(1)}, s32[4,8]{1,0:T(4,128)}, u32[]{:S(2)}) copy-start(s32[4,8]{1,0:T(4,128)} %param.24) | copy-start | bytes 388
  35.3 87.9 %copy-start.4 = (bf16[4,7168]{1,0:T(4,128)(2,1)S(1)}, bf16[4,7168]{1,0:T(4,128)(2,1)}, u32[]{:S(2)}) copy-start(bf16[4,7168]{1,0:T(4,128)(2,1)} %param.21) | copy-start | bytes 172036
  35.3 88.6 %copy-start.5 = (f32[7168]{0:T(1024)S(1)}, f32[7168]{0:T(1024)}, u32[]{:S(2)}) copy-start(f32[7168]{0:T(1024)} %param.22) | copy-start | bytes 86020
  115.9 7.3 %all-to-all-start = ((bf16[4,1,4,1792]{3,2,1,0:T(4,128)(2,1)}), bf16[4,1,4,1792]{3,2,1,0:T(4,128)(2,1)S(1)}, u32[]{:S(2)}, u32[]{:S(2)}) async-start(bf16[4,1,4,1792]{3,2,1,0:T(4,128)(2,1)} %constant_dynamic-slice_fusion), calls=%async_computation | async-start | bytes 114688 | tf_op jit(solution)/shard_map/all_to_all | solution.py:112
  119.2 54.1 %all-gather.2.cloned.1.call-start = ((), (), s32[]{:S(2)}) async-start(), calls=%async_computation.4 | async-start | bytes 3440640 | tf_op jit(solution)/shard_map/all_gather | solution.py:142
  123.3 0.7 copy-start.3
  149.1 80.6 %reduce-scatter.5.cloned.1.call-start = ((), (), s32[]{:S(2)}) async-start(), calls=%async_computation.5 | async-start | bytes 3440640
  173.3 8.6 %copy-start.2 = (bf16[2,96,7168]{2,1,0:T(8,128)(2,1)S(1)}, bf16[2,96,7168]{2,1,0:T(8,128)(2,1)}, u32[]{:S(2)}) copy-start(bf16[2,96,7168]{2,1,0:T(8,128)(2,1)} %all-gather.2.cloned.1.call-done) | copy-start | bytes 8257540
  173.3 16.4 %slice-start = ((s8[14680064]{0:T(1024)(128)(4,1)}), s8[4194304]{0:T(1024)(128)(4,1)S(1)}, s32[]{:S(2)}) async-start(s8[14680064]{0:T(1024)(128)(4,1)} %bitcast.62), calls=%async_computation.7 | async-start | bytes 8388608
  173.3 16.4 %slice-start.1 = ((s8[14680064]{0:T(1024)(128)(4,1)}), s8[4194304]{0:T(1024)(128)(4,1)S(1)}, s32[]{:S(2)}) async-start(s8[14680064]{0:T(1024)(128)(4,1)} %bitcast.62), calls=%async_computation.8 | async-start | bytes 8388608
  181.9 7.8 %slice-start.2 = ((s8[14680064]{0:T(1024)(128)(4,1)}), s8[4194304]{0:T(1024)(128)(4,1)S(1)}, s32[]{:S(2)}) async-start(s8[14680064]{0:T(1024)(128)(4,1)} %bitcast.62), calls=%async_computation.9 | async-start | bytes 8388608
  181.9 7.8 %slice-start.3 = ((s8[14680064]{0:T(1024)(128)(4,1)}), s8[2097152]{0:T(1024)(128)(4,1)S(1)}, s32[]{:S(2)}) async-start(s8[14680064]{0:T(1024)(128)(4,1)} %bitcast.62), calls=%async_computation.10 | async-start | bytes 4194304
  194.1 43.6 %copy-start.7 = (bf16[7168,16]{0,1:T(8,128)(2,1)S(1)}, bf16[7168,16]{0,1:T(8,128)(2,1)}, u32[]{:S(2)}) copy-start(bf16[7168,16]{0,1:T(8,128)(2,1)} %param.23) | copy-start | bytes 688132
  229.7 28.6 %copy-start.1 = (bf16[16,512,128]{2,1,0:T(8,128)(2,1)S(1)}, bf16[16,512,128]{2,1,0:T(8,128)(2,1)}, u32[]{:S(2)}) copy-start(bf16[16,512,128]{2,1,0:T(8,128)(2,1)} %param.19) | copy-start | bytes 6291460
  232.3 23.4 %all-to-all-start.2 = ((bf16[8,3,2,7168]{3,2,1,0:T(2,128)(2,1)}), bf16[8,3,2,7168]{3,2,1,0:T(2,128)(2,1)S(1)}, u32[]{:S(2)}, u32[]{:S(2)}) async-start(bf16[8,3,2,7168]{3,2,1,0:T(2,128)(2,1)} %bitcast.14), calls=%async_computation.2 | async-start | bytes 1376256 | tf_op jit(solution)/shard_map/all_to_all | solution.py:155
Sparse Core Ops, SparseCore 0:
  40.6 73.1 all-reduce.2
  149.2 24.1 all-gather.1
  194.3 35.3 reduce-scatter.4
